TPU v7x, 32 devices: a whole 2x2x4 slice. The times are simulated.
32 devices in a mesh: ctx: 8 (over z, y), dp: 4 (over x, core).
Axes of the slice: x: 2, y: 2, z: 4, core: 2. Of those that a mesh axis runs over, the one named last changes fastest.
Arguments:
- tokens: bfloat16 [8, 512, 4096], P('dp', 'ctx'), may hold values from -6 to 6
- queries: bfloat16 [8, 512, 2048], P('dp', 'ctx'), may hold values from -160 to 160
- d_attended: bfloat16 [8, 512, 2048], P('dp', 'ctx'), may hold values from -6 to 6
- span_order: int32 [16], replicated, may hold values from 0 to 15, each once
- norm_gain: float32 [4096], replicated, may hold values from 0.1 to 1.9
- key_weight: bfloat16 [4096, 512], replicated, may hold values from -0.09375 to 0.09375
- value_weight: bfloat16 [4096, 512], replicated, may hold values from -0.09375 to 0.09375
Outputs:
- attended: bfloat16 [8, 512, 2048], P('dp', 'ctx')
- grad_queries: bfloat16 [8, 512, 2048], P('dp', 'ctx')
- grad_tokens: bfloat16 [8, 512, 4096], P('dp', 'ctx')
- grad_key_weight: float32 [4096, 512], P(('ctx', 'dp'))
- grad_value_weight: float32 [4096, 512], P(('ctx', 'dp'))
- grad_gain: float32 [4096], P(('ctx', 'dp'))
All inputs are finite; a program needn't handle non-finite values.
Results may differ from a plain program's by a relative error of at most 0.025.
The roundings to bfloat16 on the way count: a program that leaves them out, or rounds other values in their place, can miss the bound.
Values may be sent and summed in bfloat16 or wider, within the bound.
A program may use at most 192 MiB of HBM per device.

v0:
```python
import jax
import jax.numpy as jnp
from jax import lax
from jax.sharding import PartitionSpec as P

KV_HEADS = 4
HEAD_DIM = 128
ROPE_BASE = 500000.0
EPSILON = 1e-05


def positions(span_order, span_len):
    offsets = jnp.arange(span_len, dtype=jnp.int32)
    return (span_order[:, None] * span_len + offsets[None, :]).reshape(-1)


def rotation(token_pos, head_size):
    half_dim = head_size // 2
    frequency = ROPE_BASE ** (-2.0 * jnp.arange(half_dim, dtype=jnp.float32) / head_size)
    angles = token_pos.astype(jnp.float32)[:, None] * frequency[None, :]
    angles = jnp.concatenate([angles, angles], axis=1)
    return (jnp.cos(angles), jnp.sin(angles))


def rotate_half(values):
    half_dim = values.shape[-1] // 2
    return jnp.concatenate([-values[..., half_dim:], values[..., :half_dim]], axis=-1)


def rotate_back(values):
    half_dim = values.shape[-1] // 2
    return jnp.concatenate([values[..., half_dim:], -values[..., :half_dim]], axis=-1)


def normalize(tokens, norm_gain):
    widened = tokens.astype(jnp.float32)
    rms_scale = lax.rsqrt(jnp.mean(widened * widened, axis=-1, keepdims=True) + EPSILON)
    return ((widened * rms_scale * norm_gain).astype(jnp.bfloat16), rms_scale)


def project_keys(normed, key_weight, value_weight, cosine, sine_table, kv_heads, head_size):
    row_count = normed.shape[0]
    key_pre = jnp.dot(normed, key_weight, preferred_element_type=jnp.float32).reshape(
        row_count, kv_heads, head_size
    )
    rotated = key_pre * cosine[:, None, :] + rotate_half(key_pre) * sine_table[:, None, :]
    value_rows = jnp.dot(normed, value_weight, preferred_element_type=jnp.float32)
    return (
        rotated.reshape(row_count, kv_heads * head_size).astype(jnp.bfloat16),
        value_rows.astype(jnp.bfloat16),
    )


def attend_group(query_group, grad_group, key_group, value_group, causal_mask, score_scale):
    scores = (
        jnp.einsum("tgd,sd->gts", query_group, key_group, preferred_element_type=jnp.float32)
        * score_scale
    )
    scores = jnp.where(causal_mask[None], scores, -1e30)
    row_max = jnp.max(scores, axis=-1, keepdims=True)
    exponent = jnp.exp(scores - row_max)
    probability = exponent / jnp.sum(exponent, axis=-1, keepdims=True)
    probability_b = probability.astype(jnp.bfloat16)
    attended = jnp.einsum(
        "gts,sd->tgd", probability_b, value_group, preferred_element_type=jnp.float32
    ).astype(jnp.bfloat16)
    dprob = jnp.einsum("tgd,sd->gts", grad_group, value_group, preferred_element_type=jnp.float32)
    delta = jnp.sum(grad_group.astype(jnp.float32) * attended.astype(jnp.float32), axis=-1)
    dscores = (probability * (dprob - jnp.transpose(delta)[:, :, None])).astype(jnp.bfloat16)
    dquery = (
        jnp.einsum("gts,sd->tgd", dscores, key_group, preferred_element_type=jnp.float32)
        * score_scale
    ).astype(jnp.bfloat16)
    key_term = (
        jnp.einsum("gts,tgd->sd", dscores, query_group, preferred_element_type=jnp.float32)
        * score_scale
    )
    value_term = jnp.einsum(
        "gts,tgd->sd", probability_b, grad_group, preferred_element_type=jnp.float32
    )
    return (attended, dquery, key_term, value_term)


def attend_device(queries, grads, all_keys, all_values, query_pos, key_pos, kv_heads, head_size):
    row_count = queries.shape[0]
    group_size = queries.shape[1] // (kv_heads * head_size)
    group_width = group_size * head_size
    causal_mask = key_pos[None, :] <= query_pos[:, None]
    score_scale = head_size ** (-0.5)
    outputs = []
    for head_group in range(kv_heads):
        query_group = queries[:, head_group * group_width : (head_group + 1) * group_width].reshape(
            row_count, group_size, head_size
        )
        grad_group = grads[:, head_group * group_width : (head_group + 1) * group_width].reshape(
            row_count, group_size, head_size
        )
        key_group = all_keys[:, head_group * head_size : (head_group + 1) * head_size]
        value_group = all_values[:, head_group * head_size : (head_group + 1) * head_size]
        outputs.append(
            attend_group(query_group, grad_group, key_group, value_group, causal_mask, score_scale)
        )
    attended = jnp.concatenate(
        [item[0].reshape(row_count, group_width) for item in outputs], axis=1
    )
    dquery = jnp.concatenate([item[1].reshape(row_count, group_width) for item in outputs], axis=1)
    key_terms = jnp.concatenate([item[2] for item in outputs], axis=1)
    value_terms = jnp.concatenate([item[3] for item in outputs], axis=1)
    return (attended, dquery, key_terms, value_terms)


def finish_backward(
    tokens,
    normed,
    rms_scale,
    key_grad,
    value_grad,
    cosine,
    sine_table,
    norm_gain,
    key_weight,
    value_weight,
    kv_heads,
    head_size,
):
    row_count = tokens.shape[0]
    shaped = key_grad.reshape(row_count, kv_heads, head_size)
    key_pre_grad = (
        (shaped * cosine[:, None, :] + rotate_back(shaped * sine_table[:, None, :]))
        .reshape(row_count, kv_heads * head_size)
        .astype(jnp.bfloat16)
    )
    value_pre_grad = value_grad.astype(jnp.bfloat16)
    weight_key = jnp.dot(normed.T, key_pre_grad, preferred_element_type=jnp.float32)
    weight_value = jnp.dot(normed.T, value_pre_grad, preferred_element_type=jnp.float32)
    normed_grad = jnp.dot(key_pre_grad, key_weight.T, preferred_element_type=jnp.float32) + jnp.dot(
        value_pre_grad, value_weight.T, preferred_element_type=jnp.float32
    )
    widened = tokens.astype(jnp.float32)
    gain_part = jnp.sum(normed_grad * widened * rms_scale, axis=0)
    inner_mean = jnp.mean(normed_grad * norm_gain * widened, axis=-1, keepdims=True)
    grad_rows = (
        rms_scale * norm_gain * normed_grad - widened * rms_scale**3 * inner_mean
    ).astype(jnp.bfloat16)
    return (grad_rows, weight_key, weight_value, gain_part)


def body(tokens, queries, d_attended, span_order, norm_gain, key_weight, value_weight):
    local_seqs = tokens.shape[0]
    row_count = tokens.shape[1]
    model_width = tokens.shape[2]
    kv_width = key_weight.shape[1]
    shard_index = lax.axis_index("ctx")
    token_pos = positions(span_order, row_count // 2)
    query_pos = lax.dynamic_slice_in_dim(token_pos, shard_index * row_count, row_count, 0)
    cosine, sine_table = rotation(query_pos, HEAD_DIM)
    cosine_all = jnp.tile(cosine, (local_seqs, 1))
    sine_all = jnp.tile(sine_table, (local_seqs, 1))
    flat_tokens = tokens.reshape(local_seqs * row_count, model_width)
    normed, rms_scale = normalize(flat_tokens, norm_gain)
    rotated_keys, value_rows = project_keys(
        normed, key_weight, value_weight, cosine_all, sine_all, KV_HEADS, HEAD_DIM
    )
    rotated_keys = rotated_keys.reshape(local_seqs, row_count, kv_width)
    value_rows = value_rows.reshape(local_seqs, row_count, kv_width)
    all_keys, all_values = (
        lax.all_gather(rotated_keys, "ctx", axis=1, tiled=True),
        lax.all_gather(value_rows, "ctx", axis=1, tiled=True),
    )
    attended_list, dquery_list, key_list, value_list = ([], [], [], [])
    for sequence in range(local_seqs):
        attended, dquery, key_terms, value_terms = attend_device(
            queries[sequence],
            d_attended[sequence],
            all_keys[sequence],
            all_values[sequence],
            query_pos,
            token_pos,
            KV_HEADS,
            HEAD_DIM,
        )
        attended_list.append(attended)
        dquery_list.append(dquery)
        key_list.append(key_terms)
        value_list.append(value_terms)
    key_stack = jnp.stack(key_list)
    value_stack = jnp.stack(value_list)
    key_grad, value_grad = (
        lax.psum_scatter(
            key_stack.astype(jnp.bfloat16), "ctx", scatter_dimension=1, tiled=True
        ).astype(jnp.float32),
        lax.psum_scatter(
            value_stack.astype(jnp.bfloat16), "ctx", scatter_dimension=1, tiled=True
        ).astype(jnp.float32),
    )
    key_grad = key_grad.reshape(local_seqs * row_count, kv_width)
    value_grad = value_grad.reshape(local_seqs * row_count, kv_width)
    grad_rows, weight_key, weight_value, gain_part = finish_backward(
        flat_tokens,
        normed,
        rms_scale,
        key_grad,
        value_grad,
        cosine_all,
        sine_all,
        norm_gain,
        key_weight,
        value_weight,
        KV_HEADS,
        HEAD_DIM,
    )
    weight_key, weight_value, gain_part = (
        lax.psum_scatter(
            weight_key.astype(jnp.bfloat16), "ctx", scatter_dimension=0, tiled=True
        ).astype(jnp.float32),
        lax.psum_scatter(
            weight_value.astype(jnp.bfloat16), "ctx", scatter_dimension=0, tiled=True
        ).astype(jnp.float32),
        lax.psum_scatter(
            gain_part.astype(jnp.bfloat16), "ctx", scatter_dimension=0, tiled=True
        ).astype(jnp.float32),
    )
    weight_key, weight_value, gain_part = (
        lax.psum_scatter(
            weight_key.astype(jnp.bfloat16), "dp", scatter_dimension=0, tiled=True
        ).astype(jnp.float32),
        lax.psum_scatter(
            weight_value.astype(jnp.bfloat16), "dp", scatter_dimension=0, tiled=True
        ).astype(jnp.float32),
        lax.psum_scatter(
            gain_part.astype(jnp.bfloat16), "dp", scatter_dimension=0, tiled=True
        ).astype(jnp.float32),
    )
    return (
        jnp.stack(attended_list),
        jnp.stack(dquery_list),
        grad_rows.reshape(local_seqs, row_count, model_width),
        weight_key,
        weight_value,
        gain_part,
    )


def solution(mesh):
    placed = (P("dp", "ctx", None), P("dp", "ctx", None), P("dp", "ctx", None), P(), P(), P(), P())
    return jax.shard_map(
        body,
        mesh=mesh,
        in_specs=placed,
        out_specs=(
            P("dp", "ctx", None),
            P("dp", "ctx", None),
            P("dp", "ctx", None),
            P(("ctx", "dp"), None),
            P(("ctx", "dp"), None),
            P(("ctx", "dp")),
        ),
        check_vma=False,
    )
```

profile of v0, /device:TPU:0, one launch (start us, length us, event | category | flops | bytes accessed | tf_op | source)
XLA Modules:
  0.0 512.8 jit_solution(5786807104449921285)
XLA Ops:
  10.2 6.5 %copy.154 = bf16[512,4096]{1,0:T(8,128)(2,1)} copy(bf16[512,4096]{0,1:T(8,128)(2,1)} %bitcast.753) | data formatting | bytes 8388608 | tf_op jit(solution)/shard_map/dot_general | solution.py:43
  17.0 3.4 fusion.276
  21.9 3.7 convolution_convert_fusion.1
  27.7 36.9 %all-gather.5.cloned.1.call-done = bf16[2,512,512]{2,1,0:T(8,128)(2,1)} async-done(((bf16[2,64,512]{2,1,0:T(8,128)(2,1)}), bf16[2,512,512]{2,1,0:T(8,128)(2,1)}) %all-gather.5.cloned.1.call-update) | async-done | bytes 1048592 | tf_op jit(solution)/shard_map/all_gather | solution.py:167
  65.9 1.7 fusion.264
  68.8 1.7 fusion.94
  70.5 35.8 %all-gather.3.cloned.1.call-done = bf16[2,512,512]{2,1,0:T(8,128)(2,1)} async-done(((bf16[2,64,512]{2,1,0:T(8,128)(2,1)}), bf16[2,512,512]{2,1,0:T(8,128)(2,1)}) %all-gather.3.cloned.1.call-update) | async-done | bytes 1048592 | tf_op jit(solution)/shard_map/all_gather | solution.py:168
  106.3 2.1 slice_bitcast_fusion.3
  109.8 2.0 fusion.267
  113.6 2.4 multiply_reduce_fusion.5
  116.8 2.0 fusion.270
  120.6 2.4 multiply_reduce_fusion.6
  123.9 2.4 fusion.273
  127.5 2.4 multiply_reduce_fusion.7
  130.8 2.5 fusion.252
  136.8 2.5 fusion.255
  142.8 2.4 fusion.258
  148.8 1.9 fusion.261
  163.6 2.1 copy.150
  168.1 2.1 copy.137
  172.1 99.3 %all-reduce.7.cloned.1.call-done = (bf16[2,512,512]{2,0,1:T(2,128)(2,1)}, bf16[2,512,512]{2,0,1:T(2,128)(2,1)}) async-done(((bf16[2,512,512]{2,0,1:T(2,128)(2,1)}, bf16[2,512,512]{2,0,1:T(2,128)(2,1)}), (bf16[2,512,512]{2,0,1:T(2,128)(2,1)}, bf16[2,512,512]{2,0,1:T(2,128)(2,1)})) %all-reduce.7.cloned.1.call-update) | async-done | bytes 2097168
  273.4 3.2 convolution_convert_fusion
  277.8 3.3 bitcast_convert_fusion
  283.7 1.8 copy.139
  295.8 68.7 %reduce-scatter.5.cloned.1.call-done = bf16[512,512]{1,0:T(8,128)(2,1)} async-done(((bf16[4096,512]{1,0:T(8,128)(2,1)}), bf16[512,512]{1,0:T(8,128)(2,1)}) %reduce-scatter.5.cloned.1.call-update) | async-done | bytes 524304 | tf_op jit(solution)/shard_map/reduce_scatter | solution.py:213
  364.6 3.8 fusion.277
  368.5 1.7 fusion.18
  370.2 21.3 %all-reduce.2 = bf16[4096]{0:T(1024)(128)(2,1)S(1)} all-reduce(bf16[4096]{0:T(1024)(128)(2,1)S(1)} %get-tuple-element.6), channel_id=8, replica_groups=mesh['ctx'=8,'dp'=4] {'ctx'}, use_global_device_ids=true, to_apply=%region_33.34.clone | all-reduce | flops 4096 | bytes 16384
  391.6 6.0 %all-reduce.3 = bf16[512]{0:T(512)(128)(2,1)S(1)} all-reduce(bf16[512]{0:T(512)(128)(2,1)S(1)} %dynamic-slice.5), channel_id=9, replica_groups=mesh['ctx'=8,'dp'=4] {'dp'}, use_global_device_ids=true, to_apply=%region_34.35.clone | all-reduce | flops 512 | bytes 2048
  397.7 58.8 %reduce-scatter.9.cloned.1.call-done = bf16[512,512]{1,0:T(8,128)(2,1)} async-done(((bf16[4096,512]{1,0:T(8,128)(2,1)}), bf16[512,512]{1,0:T(8,128)(2,1)}) %reduce-scatter.9.cloned.1.call-update) | async-done | bytes 524304 | tf_op jit(solution)/shard_map/reduce_scatter | solution.py:216
  458.7 21.4 %reduce-scatter.7.cloned.1.call-done = bf16[128,512]{1,0:T(8,128)(2,1)} async-done(((bf16[512,512]{1,0:T(8,128)(2,1)}), bf16[128,512]{1,0:T(8,128)(2,1)}) %reduce-scatter.7.cloned.1.call-update) | async-done | bytes 131088 | tf_op jit(solution)/shard_map/reduce_scatter | solution.py:224
  481.7 22.5 %reduce-scatter.11.cloned.1.call-done = bf16[128,512]{1,0:T(8,128)(2,1)} async-done(((bf16[512,512]{1,0:T(8,128)(2,1)}), bf16[128,512]{1,0:T(8,128)(2,1)}) %reduce-scatter.11.cloned.1.call-update) | async-done | bytes 131088 | tf_op jit(solution)/shard_map/reduce_scatter | solution.py:227
  (335 shorter events, 64.2 us)
Async XLA Ops:
  7.2 57.4 %all-gather.5.cloned.1.call-start = ((), (), s32[]{:S(2)}) async-start(), calls=%async_computation.5 | async-start | bytes 1179648 | tf_op jit(solution)/shard_map/all_gather | solution.py:167
  10.2 6.5 %copy-start = (bf16[2,64,4096]{2,1,0:T(8,128)(2,1)S(1)}, bf16[2,64,4096]{2,1,0:T(8,128)(2,1)}, u32[]{:S(2)}) copy-start(bf16[2,64,4096]{2,1,0:T(8,128)(2,1)} %param.7) | copy-start | bytes 3145732
  10.2 6.5 %copy-start.56 = (f32[4096]{0:T(1024)S(1)}, f32[4096]{0:T(1024)}, u32[]{:S(2)}) copy-start(f32[4096]{0:T(1024)} %param.11) | copy-start | bytes 49156
  21.4 84.9 %all-gather.3.cloned.1.call-start = ((), (), s32[]{:S(2)}) async-start(), calls=%async_computation.4 | async-start | bytes 1179648 | tf_op jit(solution)/shard_map/all_gather | solution.py:168
  25.6 245.8 %all-reduce.7.cloned.1.call-start = ((), (), s32[]{:S(2)}) async-start(), calls=%async_computation.10 | async-start | bytes 4194304
  26.7 39.2 %copy-start.69 = (bf16[8,4,8,128]{3,2,1,0:T(8,128)(2,1)}, bf16[8,4,8,128]{3,2,1,0:T(8,128)(2,1)S(1)}, u32[]{:S(2)}) copy-start(bf16[8,4,8,128]{3,2,1,0:T(8,128)(2,1)S(1)} %get-tuple-element.83) | copy-start | bytes 196612
  26.8 39.1 %copy-start.79 = (pred[64,512]{1,0:T(8,128)(4,1)}, pred[64,512]{1,0:T(8,128)(4,1)S(1)}, u32[]{:S(2)}) copy-start(pred[64,512]{1,0:T(8,128)(4,1)S(1)} %broadcast_compare_fusion) | copy-start | bytes 98308
  65.8 58.0 %copy-start.4 = (bf16[512,512]{1,0:T(8,128)(2,1)}, bf16[512,512]{1,0:T(8,128)(2,1)S(1)}, u32[]{:S(2)}) copy-start(bf16[512,512]{1,0:T(8,128)(2,1)S(1)} %get-tuple-element.14) | copy-start | bytes 1572868
  65.8 82.9 %copy-start.2 = (bf16[512,512]{1,0:T(8,128)(2,1)}, bf16[512,512]{1,0:T(8,128)(2,1)S(1)}, u32[]{:S(2)}) copy-start(bf16[512,512]{1,0:T(8,128)(2,1)S(1)} %get-tuple-element.15) | copy-start | bytes 1572868
  111.8 8.8 %copy-start.29 = (bf16[8,4,8,128]{3,2,1,0:T(8,128)(2,1)S(1)}, bf16[8,4,8,128]{3,2,1,0:T(8,128)(2,1)}, u32[]{:S(2)}) copy-start(bf16[8,4,8,128]{3,2,1,0:T(8,128)(2,1)} %get-tuple-element.77) | copy-start | bytes 196612
  113.5 10.3 %copy-start.65 = (bf16[8,4,8,128]{3,2,1,0:T(8,128)(2,1)S(1)}, bf16[8,4,8,128]{3,2,1,0:T(8,128)(2,1)}, u32[]{:S(2)}) copy-start(bf16[8,4,8,128]{3,2,1,0:T(8,128)(2,1)} %get-tuple-element.84) | copy-start | bytes 196612
  118.8 8.7 %copy-start.27 = (bf16[8,4,8,128]{3,2,1,0:T(8,128)(2,1)S(1)}, bf16[8,4,8,128]{3,2,1,0:T(8,128)(2,1)}, u32[]{:S(2)}) copy-start(bf16[8,4,8,128]{3,2,1,0:T(8,128)(2,1)} %get-tuple-element.80) | copy-start | bytes 196612
  120.5 10.2 %copy-start.63 = (bf16[8,4,8,128]{3,2,1,0:T(8,128)(2,1)S(1)}, bf16[8,4,8,128]{3,2,1,0:T(8,128)(2,1)}, u32[]{:S(2)}) copy-start(bf16[8,4,8,128]{3,2,1,0:T(8,128)(2,1)} %get-tuple-element.37) | copy-start | bytes 196612
  126.3 8.1 %copy-start.25 = (bf16[8,4,8,128]{3,2,1,0:T(8,128)(2,1)S(1)}, bf16[8,4,8,128]{3,2,1,0:T(8,128)(2,1)}, u32[]{:S(2)}) copy-start(bf16[8,4,8,128]{3,2,1,0:T(8,128)(2,1)} %get-tuple-element.29) | copy-start | bytes 196612
  126.3 9.1 %copy-start.6 = (bf16[512,512]{1,0:T(8,128)(2,1)S(1)}, bf16[512,512]{1,0:T(8,128)(2,1)}, u32[]{:S(2)}) copy-start(bf16[512,512]{1,0:T(8,128)(2,1)} %get-tuple-element.13) | copy-start | bytes 1572868
  127.5 9.3 %copy-start.61 = (bf16[8,4,8,128]{3,2,1,0:T(8,128)(2,1)S(1)}, bf16[8,4,8,128]{3,2,1,0:T(8,128)(2,1)}, u32[]{:S(2)}) copy-start(bf16[8,4,8,128]{3,2,1,0:T(8,128)(2,1)} %get-tuple-element.38) | copy-start | bytes 196612
  133.2 7.2 %copy-start.23 = (bf16[8,4,8,128]{3,2,1,0:T(8,128)(2,1)S(1)}, bf16[8,4,8,128]{3,2,1,0:T(8,128)(2,1)}, u32[]{:S(2)}) copy-start(bf16[8,4,8,128]{3,2,1,0:T(8,128)(2,1)} %get-tuple-element.30) | copy-start | bytes 196612
  134.4 8.4 %copy-start.59 = (bf16[8,4,8,128]{3,2,1,0:T(8,128)(2,1)S(1)}, bf16[8,4,8,128]{3,2,1,0:T(8,128)(2,1)}, u32[]{:S(2)}) copy-start(bf16[8,4,8,128]{3,2,1,0:T(8,128)(2,1)} %get-tuple-element.39) | copy-start | bytes 196612
  139.3 7.2 %copy-start.21 = (bf16[8,4,8,128]{3,2,1,0:T(8,128)(2,1)S(1)}, bf16[8,4,8,128]{3,2,1,0:T(8,128)(2,1)}, u32[]{:S(2)}) copy-start(bf16[8,4,8,128]{3,2,1,0:T(8,128)(2,1)} %get-tuple-element.31) | copy-start | bytes 196612
  140.4 8.3 %copy-start.57 = (bf16[8,4,8,128]{3,2,1,0:T(8,128)(2,1)S(1)}, bf16[8,4,8,128]{3,2,1,0:T(8,128)(2,1)}, u32[]{:S(2)}) copy-start(bf16[8,4,8,128]{3,2,1,0:T(8,128)(2,1)} %get-tuple-element.36) | copy-start | bytes 196612
  145.2 6.7 %copy-start.20 = (bf16[8,4,8,128]{3,2,1,0:T(8,128)(2,1)S(1)}, bf16[8,4,8,128]{3,2,1,0:T(8,128)(2,1)}, u32[]{:S(2)}) copy-start(bf16[8,4,8,128]{3,2,1,0:T(8,128)(2,1)} %get-tuple-element.28) | copy-start | bytes 196612
  170.2 194.3 %reduce-scatter.5.cloned.1.call-start = ((), (), s32[]{:S(2)}) async-start(), calls=%async_computation.6 | async-start | bytes 4718592 | tf_op jit(solution)/shard_map/reduce_scatter | solution.py:213
  276.7 179.8 %reduce-scatter.9.cloned.1.call-start = ((), (), s32[]{:S(2)}) async-start(), calls=%async_computation.8 | async-start | bytes 4718592 | tf_op jit(solution)/shard_map/reduce_scatter | solution.py:216
  281.1 7.6 %copy-start.3 = (bf16[512,512]{1,0:T(8,128)(2,1)S(1)}, bf16[512,512]{1,0:T(8,128)(2,1)}, u32[]{:S(2)}) copy-start(bf16[512,512]{1,0:T(8,128)(2,1)} %copy-done.2) | copy-start | bytes 1572868
  281.1 199.0 %reduce-scatter.7.cloned.1.call-start = ((), (), s32[]{:S(2)}) async-start(), calls=%async_computation.7 | async-start | bytes 655360 | tf_op jit(solution)/shard_map/reduce_scatter | solution.py:224
  286.9 6.6 %copy-start.71 = (bf16[128,4,64]{0,2,1:T(8,128)(2,1)S(1)}, bf16[128,4,64]{0,2,1:T(8,128)(2,1)}, u32[]{:S(2)}) copy-start(bf16[128,4,64]{0,2,1:T(8,128)(2,1)} %get-tuple-element.69) | copy-start | bytes 196612
  286.9 6.7 %copy-start.72 = (bf16[128,4,64]{0,2,1:T(8,128)(2,1)S(1)}, bf16[128,4,64]{0,2,1:T(8,128)(2,1)}, u32[]{:S(2)}) copy-start(bf16[128,4,64]{0,2,1:T(8,128)(2,1)} %get-tuple-element.71) | copy-start | bytes 196612
  286.9 6.7 %copy-start.73 = (bf16[128,4,64]{0,2,1:T(8,128)(2,1)S(1)}, bf16[128,4,64]{0,2,1:T(8,128)(2,1)}, u32[]{:S(2)}) copy-start(bf16[128,4,64]{0,2,1:T(8,128)(2,1)} %get-tuple-element.73) | copy-start | bytes 196612
  287.2 6.5 %copy-start.75 = (bf16[128,4,64]{0,2,1:T(8,128)(2,1)S(1)}, bf16[128,4,64]{0,2,1:T(8,128)(2,1)}, u32[]{:S(2)}) copy-start(bf16[128,4,64]{0,2,1:T(8,128)(2,1)} %get-tuple-element.61) | copy-start | bytes 196612
  287.2 6.5 %copy-start.77 = (bf16[128,4,64]{0,2,1:T(8,128)(2,1)S(1)}, bf16[128,4,64]{0,2,1:T(8,128)(2,1)}, u32[]{:S(2)}) copy-start(bf16[128,4,64]{0,2,1:T(8,128)(2,1)} %get-tuple-element.65) | copy-start | bytes 196612
  364.6 139.7 %reduce-scatter.11.cloned.1.call-start = ((), (), s32[]{:S(2)}) async-start(), calls=%async_computation.9 | async-start | bytes 655360 | tf_op jit(solution)/shard_map/reduce_scatter | solution.py:227
  368.5 88.6 %copy-start.98 = (f32[128]{0:T(128)S(1)}, f32[128]{0:T(128)}, u32[]{:S(2)}) copy-start(f32[128]{0:T(128)} %multiply_multiply_fusion) | copy-start | bytes 1540
  (76 other events, 205.5 us)
Sparse Core Ops, SparseCore 0:
  21.6 42.9 all-gather.4
  67.3 38.9 all-gather.2
  170.3 101.0 all-reduce.6
  276.8 87.6 reduce-scatter.4
  368.0 88.4 reduce-scatter.8
  458.8 21.2 reduce-scatter.6
  482.6 21.6 reduce-scatter.10
where the time goes:
time: 514 us; the launch traced here: 513 us
  waiting for transfers between devices  344 us (67%)
  matrix products  75.4 us (15%)
  blocking collectives  27.4 us (5%)
  local copies, waits for them, and re-layouts  26.2 us (5%)
  other arithmetic  21.8 us (4%)
  between operations  17.6 us (3%)
    unnamed x8, waiting for transfers between devices  99.4 us
    reduce_scatter x1, waiting for transfers between devices, body(): lax.psum_scatter(weight_key.astype(jnp.bfloat16), 'ctx', scatter_dimensio...  68.7 us
    reduce_scatter x1, waiting for transfers between devices, body(): lax.psum_scatter(weight_value.astype(jnp.bfloat16), 'ctx', scatter_dimens...  58.8 us
    all_gather x1, waiting for transfers between devices, body(): lax.all_gather(rotated_keys, 'ctx', axis=1, tiled=True)  36.9 us
    all_gather x1, waiting for transfers between devices, body(): lax.all_gather(value_rows, 'ctx', axis=1, tiled=True)  35.8 us
    unnamed x2, blocking collectives  27.4 us
    reduce_scatter x1, waiting for transfers between devices, body(): lax.psum_scatter(weight_value.astype(jnp.bfloat16), 'dp', scatter_dimensi...  22.5 us
    reduce_scatter x1, waiting for transfers between devices, body(): lax.psum_scatter(weight_key.astype(jnp.bfloat16), 'dp', scatter_dimension...  21.4 us
  transfers between devices with their start and end apart: 7, of which 7 were waited for; matrix products, arithmetic and copies ran while one was open for 8% of the time, Pallas kernels for 0%

commit v1 on v0

--- a/solution.py
+++ b/solution.py
@@ -165,7 +165,9 @@
     value_rows = value_rows.reshape(local_seqs, row_count, kv_width)
     all_keys, all_values = (
         lax.all_gather(rotated_keys, "ctx", axis=1, tiled=True),
-        lax.all_gather(value_rows, "ctx", axis=1, tiled=True),
+        jnp.concatenate(
+            lax.all_to_all(jnp.stack([value_rows] * lax.axis_size("ctx")), "ctx", 0, 0), axis=1
+        ),
     )
     attended_list, dquery_list, key_list, value_list = ([], [], [], [])
     for sequence in range(local_seqs):

time: 514 us -> 493 us (0.959)
  waiting for transfers between devices: 344 us -> 304 us
  starting transfers between devices: 0.69 us -> 8.08 us
    all_gather x1 -> x0, waiting for transfers between devices: 35.8 us -> none  [body(): lax.all_gather(value_rows, 'ctx', axis=1, tiled=True)]
    all_gather x1, waiting for transfers between devices: 36.9 us -> 27.5 us  [body(): lax.all_gather(rotated_keys, 'ctx', axis=1, tiled=True)]
    all_to_all x0 -> x1, waiting for transfers between devices: none -> 9.04 us  [body(): lax.all_to_all(jnp.stack([value_rows] * lax.axis_size('ctx')), 'ctx', 0, 0)]
    all_to_all x0 -> x1, starting transfers between devices: none -> 7.44 us  [body(): lax.all_to_all(jnp.stack([value_rows] * lax.axis_size('ctx')), 'ctx', 0, 0)]
    unnamed x8 -> x7, waiting for transfers between devices: 99.4 us -> 99.4 us
  transfers between devices with their start and end apart: 7 -> 7, of which waited for: 7 -> 7; matrix products, arithmetic and copies ran while one was open for 8% -> 10% of each run, Pallas kernels for 0% -> 0%
where the time goes in v1:
time: 493 us; the launch traced here: 491 us
  waiting for transfers between devices  304 us (62%)
  matrix products  80.2 us (16%)
  local copies, waits for them, and re-layouts  28 us (6%)
  blocking collectives  27.7 us (6%)
  other arithmetic  25.7 us (5%)
  between operations  17.6 us (4%)
  starting transfers between devices  8.08 us (2%)
    unnamed x7, waiting for transfers between devices  99.4 us
    reduce_scatter x1, waiting for transfers between devices, body(): lax.psum_scatter(weight_key.astype(jnp.bfloat16), 'ctx', scatter_dimensio...  68.7 us
    reduce_scatter x1, waiting for transfers between devices, body(): lax.psum_scatter(weight_value.astype(jnp.bfloat16), 'ctx', scatter_dimens...  57.3 us
    unnamed x2, blocking collectives  27.7 us
    all_gather x1, waiting for transfers between devices, body(): lax.all_gather(rotated_keys, 'ctx', axis=1, tiled=True)  27.5 us
    reduce_scatter x1, waiting for transfers between devices, body(): lax.psum_scatter(weight_value.astype(jnp.bfloat16), 'dp', scatter_dimensi...  22.4 us
    reduce_scatter x1, waiting for transfers between devices, body(): lax.psum_scatter(weight_key.astype(jnp.bfloat16), 'dp', scatter_dimension...  19.8 us
    sub x8, matrix products, attend_group(): exponent = jnp.exp(scores - row_max)  18.5 us
  transfers between devices with their start and end apart: 7, of which 7 were waited for; matrix products, arithmetic and copies ran while one was open for 10% of the time, Pallas kernels for 0%

profile of v1, /device:TPU:0, one launch (start us, length us, event | category | flops | bytes accessed | tf_op | source)
XLA Modules:
  0.0 491.5 jit_solution(4994864303051592058)
XLA Ops:
  10.9 2.9 convolution_convert_fusion.1
  14.9 7.4 %all-to-all-start = ((bf16[8,2,64,512]{3,2,1,0:T(8,128)(2,1)}), bf16[8,2,64,512]{3,2,1,0:T(8,128)(2,1)S(1)}, u32[]{:S(2)}, u32[]{:S(2)}) async-start(bf16[8,2,64,512]{3,2,1,0:T(8,128)(2,1)} %stack.45), calls=%async_computation | async-start | bytes 2097152 | tf_op jit(solution)/shard_map/all_to_all | solution.py:169
  24.1 6.4 %copy.154 = bf16[512,4096]{1,0:T(8,128)(2,1)} copy(bf16[512,4096]{0,1:T(8,128)(2,1)} %bitcast.752) | data formatting | bytes 8388608 | tf_op jit(solution)/shard_map/dot_general | solution.py:43
  30.5 3.4 fusion.277
  39.3 9.0 %all-to-all-done = bf16[8,2,64,512]{3,2,1,0:T(8,128)(2,1)S(1)} async-done(((bf16[8,2,64,512]{3,2,1,0:T(8,128)(2,1)}), bf16[8,2,64,512]{3,2,1,0:T(8,128)(2,1)S(1)}, u32[]{:S(2)}, u32[]{:S(2)}) %all-to-all-start) | async-done | bytes 1048608 | tf_op jit(solution)/shard_map/all_to_all | solution.py:169
  49.4 27.5 %all-gather.2.cloned.1.call-done = bf16[2,512,512]{2,1,0:T(8,128)(2,1)} async-done(((bf16[2,64,512]{2,1,0:T(8,128)(2,1)}), bf16[2,512,512]{2,1,0:T(8,128)(2,1)}) %all-gather.2.cloned.1.call-update) | async-done | bytes 1048592 | tf_op jit(solution)/shard_map/all_gather | solution.py:167
  78.1 2.6 fusion.265
  83.6 2.3 multiply_reduce_fusion.4
  85.9 2.5 fusion.268
  89.6 2.3 multiply_reduce_fusion.5
  93.7 2.5 fusion.271
  97.3 2.3 multiply_reduce_fusion.6
  101.4 2.5 fusion.274
  105.1 2.3 multiply_reduce_fusion.7
  109.1 2.5 fusion.253
  115.1 2.0 fusion.256
  121.2 2.0 fusion.259
  126.6 1.9 fusion.262
  142.1 2.1 copy.150
  146.8 2.1 copy.137
  150.8 99.3 %all-reduce.7.cloned.1.call-done = (bf16[2,512,512]{2,0,1:T(2,128)(2,1)}, bf16[2,512,512]{2,0,1:T(2,128)(2,1)}) async-done(((bf16[2,512,512]{2,0,1:T(2,128)(2,1)}, bf16[2,512,512]{2,0,1:T(2,128)(2,1)}), (bf16[2,512,512]{2,0,1:T(2,128)(2,1)}, bf16[2,512,512]{2,0,1:T(2,128)(2,1)})) %all-reduce.7.cloned.1.call-update) | async-done | bytes 2097168
  252.2 3.3 convolution_convert_fusion
  256.6 3.3 bitcast_convert_fusion
  274.6 68.7 %reduce-scatter.5.cloned.1.call-done = bf16[512,512]{1,0:T(8,128)(2,1)} async-done(((bf16[4096,512]{1,0:T(8,128)(2,1)}), bf16[512,512]{1,0:T(8,128)(2,1)}) %reduce-scatter.5.cloned.1.call-update) | async-done | bytes 524304 | tf_op jit(solution)/shard_map/reduce_scatter | solution.py:215
  343.3 3.8 fusion.278
  347.2 3.0 fusion.18
  350.2 21.7 %all-reduce.2 = bf16[4096]{0:T(1024)(128)(2,1)S(1)} all-reduce(bf16[4096]{0:T(1024)(128)(2,1)S(1)} %get-tuple-element.6), channel_id=8, replica_groups=mesh['ctx'=8,'dp'=4] {'ctx'}, use_global_device_ids=true, to_apply=%region_33.34.clone | all-reduce | flops 4096 | bytes 16384
  372.0 6.0 %all-reduce.3 = bf16[512]{0:T(512)(128)(2,1)S(1)} all-reduce(bf16[512]{0:T(512)(128)(2,1)S(1)} %dynamic-slice.5), channel_id=9, replica_groups=mesh['ctx'=8,'dp'=4] {'dp'}, use_global_device_ids=true, to_apply=%region_34.35.clone | all-reduce | flops 512 | bytes 2048
  378.0 57.3 %reduce-scatter.9.cloned.1.call-done = bf16[512,512]{1,0:T(8,128)(2,1)} async-done(((bf16[4096,512]{1,0:T(8,128)(2,1)}), bf16[512,512]{1,0:T(8,128)(2,1)}) %reduce-scatter.9.cloned.1.call-update) | async-done | bytes 524304 | tf_op jit(solution)/shard_map/reduce_scatter | solution.py:218
  435.9 3.2 fusion.15
  439.1 19.8 %reduce-scatter.7.cloned.1.call-done = bf16[128,512]{1,0:T(8,128)(2,1)} async-done(((bf16[512,512]{1,0:T(8,128)(2,1)}), bf16[128,512]{1,0:T(8,128)(2,1)}) %reduce-scatter.7.cloned.1.call-update) | async-done | bytes 131088 | tf_op jit(solution)/shard_map/reduce_scatter | solution.py:226
  460.6 22.4 %reduce-scatter.11.cloned.1.call-done = bf16[128,512]{1,0:T(8,128)(2,1)} async-done(((bf16[512,512]{1,0:T(8,128)(2,1)}), bf16[128,512]{1,0:T(8,128)(2,1)}) %reduce-scatter.11.cloned.1.call-update) | async-done | bytes 131088 | tf_op jit(solution)/shard_map/reduce_scatter | solution.py:229
  (315 shorter events, 73.4 us)
Async XLA Ops:
  13.8 8.6 %copy-start = (bf16[2,64,4096]{2,1,0:T(8,128)(2,1)S(1)}, bf16[2,64,4096]{2,1,0:T(8,128)(2,1)}, u32[]{:S(2)}) copy-start(bf16[2,64,4096]{2,1,0:T(8,128)(2,1)} %param.7) | copy-start | bytes 3145732
  13.8 8.6 %copy-start.50 = (f32[4096]{0:T(1024)S(1)}, f32[4096]{0:T(1024)}, u32[]{:S(2)}) copy-start(f32[4096]{0:T(1024)} %param.11) | copy-start | bytes 49156
  14.9 7.9 %copy-start.88 = (s32[16]{0:T(128)S(1)}, s32[16]{0:T(128)}, u32[]{:S(2)}) copy-start(s32[16]{0:T(128)} %param.10) | copy-start | bytes 196
  14.9 33.4 %all-to-all-start = ((bf16[8,2,64,512]{3,2,1,0:T(8,128)(2,1)}), bf16[8,2,64,512]{3,2,1,0:T(8,128)(2,1)S(1)}, u32[]{:S(2)}, u32[]{:S(2)}) async-start(bf16[8,2,64,512]{3,2,1,0:T(8,128)(2,1)} %stack.45), calls=%async_computation | async-start | bytes 2097152 | tf_op jit(solution)/shard_map/all_to_all | solution.py:169
  22.4 54.5 %all-gather.2.cloned.1.call-start = ((), (), s32[]{:S(2)}) async-start(), calls=%async_computation.5 | async-start | bytes 1179648 | tf_op jit(solution)/shard_map/all_gather | solution.py:167
  34.9 215.2 %all-reduce.7.cloned.1.call-start = ((), (), s32[]{:S(2)}) async-start(), calls=%async_computation.10 | async-start | bytes 4194304
  39.2 74.4 %copy-start.24 = (bf16[8,4,8,128]{3,2,1,0:T(8,128)(2,1)}, bf16[8,4,8,128]{3,2,1,0:T(8,128)(2,1)S(1)}, u32[]{:S(2)}) copy-start(bf16[8,4,8,128]{3,2,1,0:T(8,128)(2,1)S(1)} %get-tuple-element.29) | copy-start | bytes 196612
  39.2 81.0 %copy-start.22 = (bf16[8,4,8,128]{3,2,1,0:T(8,128)(2,1)}, bf16[8,4,8,128]{3,2,1,0:T(8,128)(2,1)S(1)}, u32[]{:S(2)}) copy-start(bf16[8,4,8,128]{3,2,1,0:T(8,128)(2,1)S(1)} %get-tuple-element.30) | copy-start | bytes 196612
  39.2 86.5 %copy-start.20 = (bf16[8,4,8,128]{3,2,1,0:T(8,128)(2,1)}, bf16[8,4,8,128]{3,2,1,0:T(8,128)(2,1)S(1)}, u32[]{:S(2)}) copy-start(bf16[8,4,8,128]{3,2,1,0:T(8,128)(2,1)S(1)} %get-tuple-element.31) | copy-start | bytes 196612
  39.3 92.0 %copy-start.19 = (bf16[8,4,8,128]{3,2,1,0:T(8,128)(2,1)}, bf16[8,4,8,128]{3,2,1,0:T(8,128)(2,1)S(1)}, u32[]{:S(2)}) copy-start(bf16[8,4,8,128]{3,2,1,0:T(8,128)(2,1)S(1)} %get-tuple-element.28) | copy-start | bytes 196612
  78.1 23.2 %copy-start.4 = (bf16[512,512]{1,0:T(8,128)(2,1)}, bf16[512,512]{1,0:T(8,128)(2,1)S(1)}, u32[]{:S(2)}) copy-start(bf16[512,512]{1,0:T(8,128)(2,1)S(1)} %get-tuple-element.14) | copy-start | bytes 1572868
  78.1 48.5 %copy-start.2 = (bf16[512,512]{1,0:T(8,128)(2,1)}, bf16[512,512]{1,0:T(8,128)(2,1)S(1)}, u32[]{:S(2)}) copy-start(bf16[512,512]{1,0:T(8,128)(2,1)S(1)} %get-tuple-element.15) | copy-start | bytes 1572868
  103.9 9.8 %copy-start.6 = (bf16[1,8,64,512]{3,2,0,1:T(8,128)(2,1)S(1)}, bf16[1,8,64,512]{3,2,0,1:T(8,128)(2,1)}, u32[]{:S(2)}) copy-start(bf16[1,8,64,512]{3,2,0,1:T(8,128)(2,1)} %get-tuple-element.13) | copy-start | bytes 1572868
  118.8 7.8 %copy-start.51 = (bf16[8,4,8,128]{3,2,1,0:T(8,128)(2,1)S(1)}, bf16[8,4,8,128]{3,2,1,0:T(8,128)(2,1)}, u32[]{:S(2)}) copy-start(bf16[8,4,8,128]{3,2,1,0:T(8,128)(2,1)} %get-tuple-element.36) | copy-start | bytes 196612
  123.1 8.1 %copy-start.84 = (f32[4,64]{1,0:T(4,128)}, f32[4,64]{1,0:T(4,128)S(1)}, u32[]{:S(2)}) copy-start(f32[4,64]{1,0:T(4,128)S(1)} %get-tuple-element.48) | copy-start | bytes 3076
  149.0 194.3 %reduce-scatter.5.cloned.1.call-start = ((), (), s32[]{:S(2)}) async-start(), calls=%async_computation.6 | async-start | bytes 4718592 | tf_op jit(solution)/shard_map/reduce_scatter | solution.py:215
  255.5 179.8 %reduce-scatter.9.cloned.1.call-start = ((), (), s32[]{:S(2)}) async-start(), calls=%async_computation.8 | async-start | bytes 4718592 | tf_op jit(solution)/shard_map/reduce_scatter | solution.py:218
  259.8 5.5 %copy-start.5 = (bf16[512,512]{1,0:T(8,128)(2,1)S(1)}, bf16[512,512]{1,0:T(8,128)(2,1)}, u32[]{:S(2)}) copy-start(bf16[512,512]{1,0:T(8,128)(2,1)} %copy-done.4) | copy-start | bytes 1572868
  259.8 5.8 %copy-start.9 = (bf16[4,64,512]{2,1,0:T(8,128)(2,1)S(1)}, bf16[4,64,512]{2,1,0:T(8,128)(2,1)}, u32[]{:S(2)}) copy-start(bf16[4,64,512]{2,1,0:T(8,128)(2,1)} %copy-done.8) | copy-start | bytes 786436
  259.9 6.1 %copy-start.11 = (bf16[4,64,512]{2,1,0:T(8,128)(2,1)S(1)}, bf16[4,64,512]{2,1,0:T(8,128)(2,1)}, u32[]{:S(2)}) copy-start(bf16[4,64,512]{2,1,0:T(8,128)(2,1)} %copy-done.10) | copy-start | bytes 786436
  259.9 7.6 %copy-start.3 = (bf16[512,512]{1,0:T(8,128)(2,1)S(1)}, bf16[512,512]{1,0:T(8,128)(2,1)}, u32[]{:S(2)}) copy-start(bf16[512,512]{1,0:T(8,128)(2,1)} %copy-done.2) | copy-start | bytes 1572868
  259.9 199.1 %reduce-scatter.7.cloned.1.call-start = ((), (), s32[]{:S(2)}) async-start(), calls=%async_computation.7 | async-start | bytes 655360 | tf_op jit(solution)/shard_map/reduce_scatter | solution.py:226
  265.7 6.6 %copy-start.60 = (bf16[128,4,64]{0,2,1:T(8,128)(2,1)S(1)}, bf16[128,4,64]{0,2,1:T(8,128)(2,1)}, u32[]{:S(2)}) copy-start(bf16[128,4,64]{0,2,1:T(8,128)(2,1)} %get-tuple-element.69) | copy-start | bytes 196612
  265.7 6.7 %copy-start.61 = (bf16[128,4,64]{0,2,1:T(8,128)(2,1)S(1)}, bf16[128,4,64]{0,2,1:T(8,128)(2,1)}, u32[]{:S(2)}) copy-start(bf16[128,4,64]{0,2,1:T(8,128)(2,1)} %get-tuple-element.71) | copy-start | bytes 196612
  265.7 6.7 %copy-start.62 = (bf16[128,4,64]{0,2,1:T(8,128)(2,1)S(1)}, bf16[128,4,64]{0,2,1:T(8,128)(2,1)}, u32[]{:S(2)}) copy-start(bf16[128,4,64]{0,2,1:T(8,128)(2,1)} %get-tuple-element.73) | copy-start | bytes 196612
  265.9 6.5 %copy-start.63 = (bf16[128,4,64]{0,2,1:T(8,128)(2,1)S(1)}, bf16[128,4,64]{0,2,1:T(8,128)(2,1)}, u32[]{:S(2)}) copy-start(bf16[128,4,64]{0,2,1:T(8,128)(2,1)} %get-tuple-element.75) | copy-start | bytes 196612
  265.9 6.5 %copy-start.64 = (bf16[128,4,64]{0,2,1:T(8,128)(2,1)S(1)}, bf16[128,4,64]{0,2,1:T(8,128)(2,1)}, u32[]{:S(2)}) copy-start(bf16[128,4,64]{0,2,1:T(8,128)(2,1)} %get-tuple-element.61) | copy-start | bytes 196612
  266.0 6.5 %copy-start.65 = (bf16[128,4,64]{0,2,1:T(8,128)(2,1)S(1)}, bf16[128,4,64]{0,2,1:T(8,128)(2,1)}, u32[]{:S(2)}) copy-start(bf16[128,4,64]{0,2,1:T(8,128)(2,1)} %get-tuple-element.63) | copy-start | bytes 196612
  266.0 6.5 %copy-start.66 = (bf16[128,4,64]{0,2,1:T(8,128)(2,1)S(1)}, bf16[128,4,64]{0,2,1:T(8,128)(2,1)}, u32[]{:S(2)}) copy-start(bf16[128,4,64]{0,2,1:T(8,128)(2,1)} %get-tuple-element.65) | copy-start | bytes 196612
  266.2 6.3 %copy-start.67 = (bf16[128,4,64]{0,2,1:T(8,128)(2,1)S(1)}, bf16[128,4,64]{0,2,1:T(8,128)(2,1)}, u32[]{:S(2)}) copy-start(bf16[128,4,64]{0,2,1:T(8,128)(2,1)} %get-tuple-element.67) | copy-start | bytes 196612
  343.3 139.7 %reduce-scatter.11.cloned.1.call-start = ((), (), s32[]{:S(2)}) async-start(), calls=%async_computation.9 | async-start | bytes 655360 | tf_op jit(solution)/shard_map/reduce_scatter | solution.py:229
  347.2 88.8 %copy-start.87 = (f32[128]{0:T(128)S(1)}, f32[128]{0:T(128)}, u32[]{:S(2)}) copy-start(f32[128]{0:T(128)} %multiply_multiply_fusion) | copy-start | bytes 1540
  (66 other events, 161.9 us)
Sparse Core Ops, SparseCore 0:
  35.0 41.7 all-gather.1
  149.1 100.9 all-reduce.6
  255.6 87.5 reduce-scatter.4
  346.7 88.5 reduce-scatter.8
  437.7 21.2 reduce-scatter.6
  461.3 21.6 reduce-scatter.10
